TPU v7x, 16 devices: a 4x2x1 block of a 4x4x8 slice. The times are simulated.
16 devices in a mesh: dp: 2 (over y, z), sp: 8 (over x, core).
Axes of the slice: x: 4, y: 2, z: 1, core: 2. Of those that a mesh axis runs over, the one named last changes fastest.
The devices are a block of a 4x4x8 slice.
Arguments:
- hidden: bfloat16 [256, 1280], P(('dp', 'sp')), parts along dimension 0
- seg_ids: int32 [256], P(('dp', 'sp')), parts along dimension 0
- positions: int32 [256], P(('dp', 'sp')), parts along dimension 0
- prefix_lat: bfloat16 [8192, 576], P(('dp', 'sp')), parts along dimension 0
- prefix_seg: int32 [8192], P(('dp', 'sp')), parts along dimension 0
- w_dq: bfloat16 [1280, 384], replicated
- gain_q: bfloat16 [384], replicated
- w_uq: bfloat16 [384, 6144], replicated
- w_dkv: bfloat16 [1280, 576], replicated
- gain_kv: bfloat16 [512], replicated
- w_ukv: bfloat16 [512, 8192], replicated
- w_o: bfloat16 [4096, 1280], replicated
Outputs:
- output: bfloat16 [256, 1280], P(('dp', 'sp')), parts along dimension 0
There are 2 independent parts. A program takes and returns all parts, laid end to end along the dimension named above; an argument that names none is the same for every part.
All inputs are finite; a program needn't handle non-finite values.
Results may differ from a plain program's by a relative error of at most 0.00489144.
Values are sent between devices in bfloat16 or wider.
A program may use at most 768 MiB of HBM per device.

v0:
```python
import jax
import jax.numpy as jnp
from jax import lax
from jax.sharding import PartitionSpec as P

KV_LAT = 512
ROPE_DIM = 64
NOPE_DIM = 128
V_DIM = 128
QK_DIM = NOPE_DIM + ROPE_DIM
KV_HEAD = NOPE_DIM + V_DIM
ROW_BUDGET = 2048
EPS = 1e-6
ROPE_BASE = 10000.0
NEG_BIG = -1e30


def rms_norm(values, gain):
    inv_rms = lax.rsqrt(jnp.mean(values * values, axis=-1, keepdims=True) + EPS)
    return values * inv_rms * gain.astype(jnp.float32)


def rope_tables(positions):
    half_dim = ROPE_DIM // 2
    inv_freq = ROPE_BASE ** (-jnp.arange(half_dim, dtype=jnp.float32) / half_dim)
    angles = positions.astype(jnp.float32)[:, None] * inv_freq[None, :]
    return jnp.cos(angles), jnp.sin(angles)


def rope_apply(values, cos_t, sin_t):
    half_dim = ROPE_DIM // 2
    lower_half = values[..., :half_dim]
    upper_half = values[..., half_dim:]
    return jnp.concatenate([lower_half * cos_t - upper_half * sin_t, upper_half * cos_t + lower_half * sin_t], axis=-1)


def latent_stage(hidden, positions, w_dq, gain_q, w_dkv, gain_kv):
    q_lat = rms_norm(jnp.dot(hidden, w_dq, preferred_element_type=jnp.float32), gain_q).astype(jnp.bfloat16)
    kv_down = jnp.dot(hidden, w_dkv, preferred_element_type=jnp.float32)
    cos_t, sin_t = rope_tables(positions)
    kv_lat = rms_norm(kv_down[:, :KV_LAT], gain_kv).astype(jnp.bfloat16)
    key_rope = rope_apply(kv_down[:, KV_LAT:], cos_t, sin_t).astype(jnp.bfloat16)
    return q_lat, jnp.concatenate([kv_lat, key_rope], axis=1)


def head_attention(q_lat, q_pos, q_seg, key_lat, key_seg, key_pos, w_uq_part, w_ukv_part, head_count):
    tokens = q_lat.shape[0]
    q_full = jnp.einsum("tc,chd->thd", q_lat, w_uq_part.reshape(-1, head_count, QK_DIM), preferred_element_type=jnp.float32)
    cos_t, sin_t = rope_tables(q_pos)
    q_nope = q_full[..., :NOPE_DIM].astype(jnp.bfloat16)
    q_rope = rope_apply(q_full[..., NOPE_DIM:], cos_t[:, None, :], sin_t[:, None, :]).astype(jnp.bfloat16)
    kv_up = jnp.einsum("kc,chd->khd", key_lat[:, :KV_LAT], w_ukv_part.reshape(KV_LAT, head_count, KV_HEAD), preferred_element_type=jnp.float32).astype(jnp.bfloat16)
    k_nope = kv_up[..., :NOPE_DIM]
    v_heads = kv_up[..., NOPE_DIM:]
    k_rope = key_lat[:, KV_LAT:]
    q_block = min(tokens, max(1, ROW_BUDGET // head_count))
    n_blocks = tokens // q_block

    def attend(block):
        qn_blk, qr_blk, seg_blk, pos_blk = block
        scores = jnp.einsum("qhd,khd->hqk", qn_blk, k_nope, preferred_element_type=jnp.float32)
        scores = scores + jnp.einsum("qhd,kd->hqk", qr_blk, k_rope, preferred_element_type=jnp.float32)
        allowed = (seg_blk[:, None] == key_seg[None, :]) & (key_pos[None, :] <= pos_blk[:, None])
        scores = jnp.where(allowed[None], scores * QK_DIM ** -0.5, NEG_BIG)
        probs = jax.nn.softmax(scores, axis=-1).astype(jnp.bfloat16)
        return jnp.einsum("hqk,khd->qhd", probs, v_heads, preferred_element_type=jnp.float32).astype(jnp.bfloat16)

    block_outs = lax.map(attend, (q_nope.reshape(n_blocks, q_block, head_count, NOPE_DIM), q_rope.reshape(n_blocks, q_block, head_count, ROPE_DIM), q_seg.reshape(n_blocks, q_block), q_pos.reshape(n_blocks, q_block)))
    return block_outs.reshape(tokens, head_count * V_DIM)


def solution(mesh):
    group_size = mesh.shape["sp"]
    tok_spec = P(("dp", "sp"), None)
    vec_spec = P(("dp", "sp"))
    mat_spec = P(None, None)
    gain_spec = P(None)

    def device_step(hidden, seg_ids, positions, prefix_lat, prefix_seg, w_dq, gain_q, w_uq, w_dkv, gain_kv, w_ukv, w_o):
        q_width = w_dq.shape[1]
        head_dev = w_o.shape[0] // V_DIM // group_size
        q_lat, new_lat = latent_stage(hidden, positions, w_dq, gain_q, w_dkv, gain_kv)
        gathered = lax.all_gather(jnp.concatenate([q_lat, new_lat], axis=1), "sp", axis=0, tiled=True)
        prefix_all = lax.all_gather(prefix_lat, "sp", axis=0, tiled=True)
        seg_all = lax.all_gather(seg_ids, "sp", axis=0, tiled=True)
        pos_all = lax.all_gather(positions, "sp", axis=0, tiled=True)
        prefix_seg_all = lax.all_gather(prefix_seg, "sp", axis=0, tiled=True)
        first_head = lax.axis_index("sp") * head_dev
        w_uq_mine = lax.dynamic_slice_in_dim(w_uq, first_head * QK_DIM, head_dev * QK_DIM, axis=1)
        w_ukv_mine = lax.dynamic_slice_in_dim(w_ukv, first_head * KV_HEAD, head_dev * KV_HEAD, axis=1)
        key_lat = jnp.concatenate([prefix_all, gathered[:, q_width:]], axis=0)
        key_seg = jnp.concatenate([prefix_seg_all, seg_all])
        key_pos = jnp.concatenate([jnp.full(prefix_seg_all.shape, -1, jnp.int32), pos_all])
        heads_out = head_attention(gathered[:, :q_width], pos_all, seg_all, key_lat, key_seg, key_pos, w_uq_mine, w_ukv_mine, head_dev)
        tok_out = lax.all_to_all(heads_out, "sp", 0, 1, tiled=True)
        return jnp.dot(tok_out, w_o, preferred_element_type=jnp.float32).astype(jnp.bfloat16)

    return jax.shard_map(
        device_step,
        mesh=mesh,
        in_specs=(tok_spec, vec_spec, vec_spec, tok_spec, vec_spec, mat_spec, gain_spec, mat_spec, mat_spec, gain_spec, mat_spec, mat_spec),
        out_specs=tok_spec,
        check_vma=False,
    )
```

profile of v0, /device:TPU:112, one launch (start us, length us, event | category | flops | bytes accessed | tf_op | source)
XLA Modules:
  0.0 126.5 jit_solution(18417403175212486424)
XLA Ops:
  6.6 2.3 %copy.29 = bf16[512,576]{1,0:T(8,128)(2,1)} copy(bf16[512,576]{0,1:T(8,128)(2,1)} %param.15) | data formatting | bytes 1179648 | tf_op args[3]
  8.8 0.1 all-gather.3.cloned.1.call-update
  8.9 0.7 convert_element_type.42
  9.5 1.2 dynamic-slice.4
  11.4 0.9 dynamic-update-slice.1
  12.3 0.8 dynamic-update-slice
  13.1 10.5 %all-reduce.3 = (s32[128]{0:T(128)S(1)}, s32[128]{0:T(128)S(1)}) all-reduce(s32[128]{0:T(128)S(1)} %dynamic-update-slice.1, s32[128]{0:T(128)S(1)} %dynamic-update-slice), channel_id=1, replica_groups=mesh['dp'=2,'sp'=8] {'sp'}, use_global_device_ids=true, to_apply=%add.2 | all-reduce | flops 256 | bytes 2048
  23.6 0.7 convert_element_type.38
  24.3 0.7 convert_element_type.40
  25.0 1.3 %fusion.39 = f32[16,576]{1,0:T(8,128)S(1)} fusion(bf16[16,1280]{1,0:T(8,128)(2,1)} %param.12, bf16[1280,576]{0,1:T(8,128)(2,1)S(1)} %copy-done), kind=kOutput, calls=%fused_computation.58 | convolution fusion | flops 23592960 | bytes 1552384 | tf_op jit(solution)/shard_map/dot_general | solution.py:39
  26.3 0.1 multiply_reduce_fusion
  26.4 1.6 %multiply_reduce_fusion.1 = (f32[16]{0:T(128)S(1)}, f32[16,384]{1,0:T(8,128)S(1)}) fusion(bf16[16,1280]{1,0:T(8,128)(2,1)} %param.12, bf16[1280,384]{1,0:T(8,128)(2,1)} %param.17), kind=kOutput, calls=%fused_computation.36 | convolution fusion | flops 15740912 | bytes 1048640 | tf_op jit(solution)/shard_map/dot_general | solution.py:38
  28.0 0.1 fusion.32
  28.1 0.1 multiply_convert_fusion.1
  28.2 0.1 multiply_convert_fusion
  28.3 0.1 pad_maximum_fusion.1
  28.4 21.5 %all_gather.16 = bf16[128,960]{1,0:T(8,128)(2,1)S(1)} all-gather(bf16[16,960]{1,0:T(8,128)(2,1)S(1)} %pad_maximum_fusion.1), channel_id=1, replica_groups=mesh['dp'=2,'sp'=8] {'sp'}, dimensions={0}, use_global_device_ids=true | all-gather | bytes 276480 | tf_op jit(solution)/shard_map/all_gather | solution.py:83
  49.9 1.3 %constant_dynamic-slice_fusion = bf16[512,1024]{1,0:T(8,128)(2,1)S(1)} fusion(bf16[512,8192]{1,0:T(8,128)(2,1)} %param.22, s32[]{:T(128)S(6)} %select_n.11), kind=kLoop, calls=%fused_computation.51 | loop fusion | bytes 2097156 | tf_op jit(solution)/shard_map/dynamic_slice | solution.py:90
  51.2 0.5 copy.45
  51.8 23.2 %all-gather = s32[8,1,512]{2,1,0:T(1,128)S(1)} all-gather(s32[1,1,512]{2,1,0:T(1,128)S(1)} %bitcast.39), channel_id=1, replica_groups=mesh['dp'=2,'sp'=8] {'sp'}, dimensions={0}, use_global_device_ids=true | all-gather | bytes 18432 | tf_op jit(solution)/shard_map/all_gather | solution.py:87
  75.0 0.1 multiply_cosine_fusion
  75.2 1.4 %fusion.21 = f32[128,768]{0,1:S(1)} fusion(bf16[384,6144]{1,0:T(8,128)(2,1)} %param.19, s32[]{:T(128)S(6)} %select_n.12, bf16[128,960]{1,0:T(8,128)(2,1)S(1)} %all_gather.16), kind=kOutput, calls=%fused_computation.23 | convolution fusion | flops 75497472 | bytes 1081348
  76.7 0.5 compare_and_fusion
  77.2 10.3 %convolution_convert_fusion = bf16[4224,4,256]{2,0,1:T(8,128)(2,1)} fusion(bf16[512,4,256]{0,2,1:T(8,128)(2,1)S(1)} %bitcast.35, bf16[4096,576]{1,0:T(8,128)(2,1)} %all-gather.3.cloned.1.call-done, bf16[128,576]{1,0:T(8,128)(2,1)S(1)} %slice.58), kind=kOutput, calls=%fused_computation.2 | convolution fusion | flops 4442161152 | bytes 14565376 | tf_op jit(solution)/shard_map/kc,chd->khd/dot_general | solution.py:52
  87.5 1.3 %fusion.18 = f32[4224,128,4]{0,1,2:T(8,128)S(1)} fusion(bf16[128,576]{1,0:T(8,128)(2,1)S(1)} %slice.58, bf16[4096,576]{1,0:T(8,128)(2,1)S(1)} %copy-done.2, bf16[128,4,32]{0,2,1:T(8,128)(2,1)S(1)} %get-tuple-element.28, bf16[128,4,32]{0,2,1:T(8,128)(2,1)S(1)} %get-tuple-element.27), kind=kOutput, calls=%fused_computation.21 | convolution fusion | flops 278036480 | bytes 13582336 | tf_op jit(solution)/shard_map/while/body/eval_jaxpr/qhd,kd->hqk/dot_general | solution.py:62
  88.9 4.2 %fusion.3 = f32[4,128,4224]{2,1,0:T(8,128)S(1)} fusion(f32[4224,128,4]{0,1,2:T(8,128)S(1)} %fusion.18, bf16[4224,4,256]{2,0,1:T(8,128)(2,1)} %convolution_convert_fusion, pred[128,4224]{1,0:T(8,128)(4,1)S(1)} %compare_and_fusion, f32[128,4,192]{0,2,1:T(8,128)S(1)} %bitcast.34), kind=kOutput, calls=%fused_computation.5 | convolution fusion | flops 560136192 | bytes 22298624 | tf_op jit(solution)/shard_map/while/body/eval_jaxpr/qhd,khd->hqk/dot_general | solution.py:61
  93.1 4.8 %fusion.38 = (f32[4,128]{1,0:T(4,128)S(1)}, f32[4,128,4224]{2,1,0:T(8,128)}) fusion(f32[4,128,4224]{2,1,0:T(8,128)S(1)} %fusion.3), kind=kOutput, calls=%fused_computation.57 | output fusion | flops 4329599 | bytes 17303552 | tf_op jit(solution)/shard_map/while/body/eval_jaxpr/sub | solution.py:65
  97.9 6.6 %fusion.14 = bf16[128,4,128]{0,2,1:T(8,128)(2,1)S(1)} fusion(f32[4,128,4224]{2,1,0:T(8,128)} %get-tuple-element.49, f32[4,128]{1,0:T(4,128)S(1)} %get-tuple-element.48, bf16[4224,4,256]{2,0,1:T(8,128)(2,1)} %convolution_convert_fusion), kind=kOutput, calls=%fused_computation.18 | convolution fusion | flops 558039040 | bytes 13109248 | tf_op jit(solution)/shard_map/while/body/eval_jaxpr/hqk,khd->qhd/dot_general | solution.py:66
  104.6 0.1 copy.37
  104.7 0.1 all_to_all.14
  104.8 8.7 %all_to_all.19 = bf16[8,16,512]{2,1,0:T(8,128)(2,1)S(1)} all-to-all(bf16[8,16,512]{2,1,0:T(8,128)(2,1)S(1)} %all_to_all.14), channel_id=1, replica_groups=mesh['dp'=2,'sp'=8] {'sp'}, dimensions={0} | all-to-all | bytes 262144 | tf_op jit(solution)/shard_map/all_to_all | solution.py:95
  113.5 6.2 %convolution_convert_fusion.1 = bf16[16,1280]{1,0:T(8,128)(2,1)} fusion(bf16[16,4096]{1,0:T(8,128)(2,1)S(1)} %bitcast.36, bf16[4096,1280]{1,0:T(8,128)(2,1)} %param.23), kind=kOutput, calls=%fused_computation.15 | convolution fusion | flops 167792640 | bytes 10657792 | tf_op jit(solution)/shard_map/dot_general | solution.py:96
  (21 shorter events, 0.1 us)
Async XLA Ops:
  6.5 18.4 %copy-start = (bf16[1280,576]{0,1:T(8,128)(2,1)S(1)}, bf16[1280,576]{0,1:T(8,128)(2,1)}, u32[]{:S(2)}) copy-start(bf16[1280,576]{0,1:T(8,128)(2,1)} %param.20) | copy-start | bytes 4423684
  6.6 45.2 %copy-start.3 = (s32[512]{0:T(512)S(1)}, s32[512]{0:T(512)}, u32[]{:S(2)}) copy-start(s32[512]{0:T(512)} %param.16) | copy-start | bytes 6148
  6.6 70.6 %all-gather.3.cloned.1.call-start = ((), (), s32[]{:S(2)}) async-start(), calls=%async_computation.1 | async-start | bytes 5898240 | tf_op jit(solution)/shard_map/all_gather | solution.py:84
  77.2 10.3 %copy-start.2 = (bf16[4096,576]{1,0:T(8,128)(2,1)S(1)}, bf16[4096,576]{1,0:T(8,128)(2,1)}, u32[]{:S(2)}) copy-start(bf16[4096,576]{1,0:T(8,128)(2,1)} %all-gather.3.cloned.1.call-done) | copy-start | bytes 14155780
  113.4 6.2 %copy-start.1 = (bf16[1280,576]{0,1:T(8,128)(2,1)S(1)}, bf16[1280,576]{0,1:T(8,128)(2,1)}, u32[]{:S(2)}) copy-start(bf16[1280,576]{0,1:T(8,128)(2,1)} %param.20) | copy-start | bytes 4423684
Sparse Core Ops, SparseCore 0:
  9.0 35.7 all-gather.2
where the time goes:
time: 127 us; the launch traced here: 126 us
  blocking collectives  63.9 us (50%)
  matrix products  33 us (26%)
  between operations  14.2 us (11%)
  other arithmetic  8 us (6%)
  local copies, waits for them, and re-layouts  7.28 us (6%)
    all_gather x1, blocking collectives, device_step(): prefix_seg_all = lax.all_gather(prefix_seg, 'sp', axis=0, tiled=True)  23.2 us
    all_gather x1, blocking collectives, device_step(): lax.all_gather(jnp.concatenate([q_lat, new_lat], axis=1), 'sp', axis=0, t...  21.5 us
    unnamed x1, blocking collectives  10.5 us
    dot_general x1, matrix products, head_attention(): jnp.einsum('kc,chd->khd', key_lat[:, :KV_LAT], w_ukv_part.reshape(KV_LAT,...  10.3 us
    all_to_all x1, blocking collectives, device_step(): tok_out = lax.all_to_all(heads_out, 'sp', 0, 1, tiled=True)  8.65 us
    dot_general x1, matrix products, attend(): jnp.einsum('hqk,khd->qhd', probs, v_heads, preferred_element_type=jnp.flo...  6.64 us
    dot_general x1, matrix products, device_step(): jnp.dot(tok_out, w_o, preferred_element_type=jnp.float32)  6.18 us
    unnamed x15, local copies, waits for them, and re-layouts  5.75 us
  transfers between devices with their start and end apart: 1, of which 0 were waited for; matrix products, arithmetic and copies ran while one was open for 10% of the time, Pallas kernels for 0%

commit v1 on v0

v1 whole, which is shorter than its diff:
```python
import functools
import math

import jax
import jax.numpy as jnp
import numpy as np
from jax import lax
from jax.experimental import pallas as pl
from jax.experimental.pallas import tpu as pltpu
from jax.sharding import PartitionSpec as P

ROPE_DIM = 64
HALF = ROPE_DIM // 2
NOPE_DIM = 128
V_DIM = 128
QK_DIM = NOPE_DIM + ROPE_DIM
KV_HEAD = NOPE_DIM + V_DIM
CORES = 2
EPS = 1e-6
ROPE_BASE = 10000.0
NEG_BIG = -1e30
EXP_SCALE = QK_DIM ** -0.5 * math.log2(math.e)
LANES = 128
N_CHUNK = 256
KV_LOADS = 4

F32 = jnp.float32
BF16 = jnp.bfloat16


def dot(a, b):
    return jnp.dot(a, b, preferred_element_type=F32)


def dot_nt(a, b):
    return lax.dot_general(a, b, (((1,), (1,)), ((), ())), preferred_element_type=F32)


def dot_tn(a, b):
    return lax.dot_general(a, b, (((0,), (0,)), ((), ())), preferred_element_type=F32)


def rms_norm(values, gain):
    inv_rms = lax.rsqrt(jnp.mean(values * values, axis=-1, keepdims=True) + EPS)
    return values * inv_rms * gain.astype(F32)


def row_to_column(row):
    size = row.shape[1]
    here = lax.broadcasted_iota(jnp.int32, (size, size), 0) == lax.broadcasted_iota(jnp.int32, (size, size), 1)
    return jnp.sum(jnp.where(here, jnp.broadcast_to(row, (size, size)), 0.0), axis=1, keepdims=True)


def seg_lanes(seg_column):
    lane = lax.broadcasted_iota(jnp.int32, (seg_column.shape[0], ROPE_DIM), 1).astype(F32)
    return seg_column == lane


def kernel(
    n,
    freq_ref, seg_ref, pos_ref, pseg_ref, gain_q_ref, gain_kv_ref,
    hid_hbm, pre_hbm, wdq_hbm, wuq_hbm, wdkv_hbm, wukv_hbm, wo_hbm,
    out_ref,
    hid_v, wdq_v, wdkv_v, wuq_v, wukv_v, wo_v,
    lat, pseg_mate, qlat_all, meta_all, key_tail, keys, queries, probs,
    stats, stats_rx, acc, split, bias, y_mine, y_out, y_rx, z, z_rx,
    load_sem, ukv_sem, mate_send, mate_recv, gat_send, gat_recv, met_send, met_recv,
    st_send, st_recv, pair_send, pair_recv, red_send, red_recv,
):
    me = lax.axis_index("sp")
    core = lax.rem(me, CORES)
    chip = lax.div(me, CORES)
    chips = n // CORES
    mate = chip * CORES + (CORES - 1 - core)
    toks = hid_v.shape[0]
    pre = pre_hbm.shape[0]
    kv_lat = wukv_v.shape[0]
    heads = keys.shape[0]
    rows = lat.shape[0]
    old = CORES * pre

    def load(src, dst, i):
        copy = pltpu.make_async_copy(src, dst, load_sem.at[i])
        copy.start()
        return copy

    load_hid = load(hid_hbm, hid_v, 0)
    load_dq = load(wdq_hbm, wdq_v, 1)
    load_dkv = load(wdkv_hbm, wdkv_v, 2)
    load_pre = load(pre_hbm, lat.at[pl.ds(0, pre)], 3)
    kv_cols = heads * KV_HEAD
    part = kv_cols // KV_LOADS
    load_ukv = []
    for i in range(KV_LOADS):
        copy = pltpu.make_async_copy(
            wukv_hbm.at[:, pl.ds(pl.multiple_of(core * kv_cols + i * part, LANES), part)],
            wukv_v.at[:, pl.ds(i * part, part)],
            ukv_sem.at[i],
        )
        copy.start()
        load_ukv.append(copy)

    barrier = pltpu.get_barrier_semaphore()
    for j in range(1, n):
        pl.semaphore_signal(barrier, inc=1, device_id={"sp": lax.rem(me + j, n)}, device_id_type=pl.DeviceIdType.MESH)
    pl.semaphore_wait(barrier, n - 1)

    def send(src, dst, send_sem, recv_sem, target):
        copy = pltpu.make_async_remote_copy(
            src_ref=src, dst_ref=dst, send_sem=send_sem, recv_sem=recv_sem,
            device_id={"sp": target}, device_id_type=pl.DeviceIdType.MESH,
        )
        copy.start()
        return copy

    send_pre = send(pre_hbm, lat.at[pl.ds(pre, pre)], mate_send.at[0], mate_recv.at[0], mate)
    send_pseg = send(pseg_ref, pseg_mate, mate_send.at[1], mate_recv.at[1], mate)

    pos_col = row_to_column(pos_ref[...].astype(F32))
    seg_col = row_to_column(seg_ref[...].astype(F32))
    angles = pos_col * freq_ref[...]
    lane = lax.broadcasted_iota(jnp.int32, (toks, LANES), 1)
    cos_t = jnp.cos(angles)
    sin_t = jnp.sin(angles)
    meta = jnp.where(lane < HALF, cos_t, jnp.where(lane < 2 * HALF, sin_t, jnp.where(lane == 2 * HALF, seg_col, pos_col)))
    my_rows = pl.ds(pl.multiple_of(me * toks, toks), toks)
    meta_all[my_rows, :] = meta

    load_hid.wait()
    load_dq.wait()
    qlat_all[my_rows, :] = rms_norm(dot(hid_v[...], wdq_v[...]), gain_q_ref[...]).astype(BF16)
    gathers = []
    for j in range(1, n):
        target = lax.rem(me + j, n)
        gathers.append(send(qlat_all.at[my_rows], qlat_all.at[my_rows], gat_send.at[j - 1], gat_recv.at[j - 1], target))
        gathers.append(send(meta_all.at[my_rows], meta_all.at[my_rows], met_send.at[j - 1], met_recv.at[j - 1], target))

    load_dkv.wait()
    down = dot(hid_v[...], wdkv_v[...])
    c_kv = rms_norm(down[:, :kv_lat], gain_kv_ref[...])
    low, high = down[:, kv_lat:kv_lat + HALF], down[:, kv_lat + HALF:]
    cos_m, sin_m = cos_t[:, :HALF], sin_t[:, :HALF]
    k_new = jnp.concatenate([low * cos_m - high * sin_m, high * cos_m + low * sin_m], axis=1)
    lat[pl.ds(old, toks), :] = jnp.concatenate([c_kv, k_new], axis=1).astype(BF16)
    send_new = send(lat.at[pl.ds(old, toks)], lat.at[pl.ds(old + toks, toks)], mate_send.at[2], mate_recv.at[2], mate)

    load_uq = load(wuq_hbm.at[:, pl.ds(pl.multiple_of(core * heads * QK_DIM, LANES), heads * QK_DIM)], wuq_v, 4)
    load_o = load(wo_hbm.at[pl.ds(pl.multiple_of(core * heads * V_DIM, LANES), heads * V_DIM)], wo_v, 5)

    def pair_weights(pair, offset):
        first = pl.multiple_of(pair * (2 * KV_HEAD) + offset, LANES)
        second = pl.multiple_of(pair * (2 * KV_HEAD) + KV_HEAD + offset, LANES)
        return jnp.concatenate([wukv_v[:, pl.ds(first, LANES)], wukv_v[:, pl.ds(second, LANES)]], axis=1)

    def raise_keys(start, size):
        def step(pair, carry):
            up = dot(lat[pl.ds(start, size), :kv_lat], pair_weights(pair, 0)).astype(BF16)
            keys[2 * pair, pl.ds(start, size), :] = up[:, :NOPE_DIM]
            keys[2 * pair + 1, pl.ds(start, size), :] = up[:, NOPE_DIM:]
            return carry
        return step

    load_pre.wait()
    pairs_per_load = heads // 2 // KV_LOADS
    for i in range(KV_LOADS):
        load_ukv[i].wait()
        lax.fori_loop(i * pairs_per_load, (i + 1) * pairs_per_load, raise_keys(0, pre), 0)
    send_pre.wait_recv()
    send_pseg.wait_recv()
    send_new.wait_recv()
    lax.fori_loop(0, heads // 2, raise_keys(pre, rows - pre), 0)

    def prefix_column(ref):
        wide = jnp.broadcast_to(ref[...].astype(F32), (8, pre))
        return jnp.transpose(wide)[:, :1]

    def put_tail(start, size, seg_column):
        rope = lat[pl.ds(start, size), kv_lat:].astype(F32)
        tail = jnp.concatenate([rope, jnp.where(seg_lanes(seg_column), 1.0, 0.0)], axis=1)
        key_tail[pl.ds(start, size), :] = tail.astype(BF16)

    put_tail(0, pre, prefix_column(pseg_ref))
    put_tail(pre, pre, prefix_column(pseg_mate))

    for copy in gathers:
        copy.wait_recv()
    mate_rows = pl.ds(pl.multiple_of(mate * toks, toks), toks)
    new_meta = jnp.concatenate([meta_all[my_rows, :], meta_all[mate_rows, :]], axis=0)
    put_tail(old, CORES * toks, new_meta[:, 2 * HALF:2 * HALF + 1])
    every = meta_all[...]
    q_pos = jnp.transpose(every)[2 * HALF + 1:2 * HALF + 2, :]
    bias[...] = jnp.where(new_meta[:, 2 * HALF + 1:2 * HALF + 2] <= q_pos, 0.0, NEG_BIG)

    load_uq.wait()
    q_mask = jnp.where(seg_lanes(every[:, 2 * HALF:2 * HALF + 1]), 0.0, NEG_BIG)
    cos_a, sin_a = every[:, :HALF], every[:, HALF:2 * HALF]
    cos_q = jnp.concatenate([cos_a, cos_a], axis=1)
    sin_q = jnp.concatenate([-sin_a, sin_a], axis=1)

    def put_query(head, nope, u):
        turned = jnp.concatenate([u[:, HALF:], u[:, :HALF]], axis=1)
        tail = jnp.concatenate([u * cos_q + turned * sin_q, q_mask], axis=1)
        queries[head] = jnp.concatenate([nope.astype(BF16), tail.astype(BF16)], axis=1)

    def raise_queries(pair, carry):
        cols = pl.ds(pl.multiple_of(pair * (2 * QK_DIM), LANES), 2 * QK_DIM)
        q = dot(qlat_all[...], wuq_v[:, cols])
        put_query(2 * pair, q[:, :NOPE_DIM], q[:, NOPE_DIM:QK_DIM])
        put_query(2 * pair + 1, q[:, QK_DIM:QK_DIM + NOPE_DIM], q[:, QK_DIM + NOPE_DIM:])
        return carry

    lax.fori_loop(0, heads // 2, raise_queries, 0)

    def score(head, carry):
        k_full = jnp.concatenate([keys[head], key_tail[...]], axis=1)
        s = dot_nt(k_full, queries[head])
        s_old, s_new = s[:old], s[old:] + bias[...]
        top = jnp.maximum(jnp.max(s_old, axis=0, keepdims=True), jnp.max(s_new, axis=0, keepdims=True))
        p_old = jnp.exp2((s_old - top) * EXP_SCALE)
        p_new = jnp.exp2((s_new - top) * EXP_SCALE)
        probs[head, :old, :] = p_old.astype(BF16)
        probs[head, old:, :] = p_new.astype(BF16)
        stats[pl.ds(head, 1), :] = top
        stats[pl.ds(heads + head, 1), :] = jnp.sum(p_old, axis=0, keepdims=True) + jnp.sum(p_new, axis=0, keepdims=True)
        return carry

    lax.fori_loop(0, heads, score, 0)

    def peer(j):
        return lax.rem(chip + j, chips)

    send_stats = [
        send(stats, stats_rx.at[j - 1], st_send.at[j - 1], st_recv.at[j - 1], peer(j) * CORES + core)
        for j in range(1, chips)
    ]

    def attend(pair, carry):
        v = dot(lat[:, :kv_lat], pair_weights(pair, NOPE_DIM)).astype(BF16)
        for i in range(2):
            cols = pl.ds(pl.multiple_of((2 * pair + i) * V_DIM, LANES), V_DIM)
            acc[:, cols] = dot_tn(probs[2 * pair + i], v[:, i * V_DIM:(i + 1) * V_DIM])
        return carry

    lax.fori_loop(0, heads // 2, attend, 0)

    for copy in send_stats:
        copy.wait_recv()
    tops = [stats[:heads, :]] + [stats_rx[j, :heads, :] for j in range(chips - 1)]
    sums = [stats[heads:, :]] + [stats_rx[j, heads:, :] for j in range(chips - 1)]
    top = functools.reduce(jnp.maximum, tops)
    shares = [jnp.exp2((t - top) * EXP_SCALE) for t in tops]
    total = functools.reduce(jnp.add, [s * w for s, w in zip(sums, shares)])
    scale = jnp.transpose(shares[0] / total)
    all_toks = n * toks
    for head in range(heads):
        cols = pl.ds(head * V_DIM, V_DIM)
        o = acc[:, cols] * scale[:, head:head + 1]
        o_hi = o.astype(BF16)
        split[:all_toks, cols] = o_hi
        split[all_toks:, cols] = (o - o_hi.astype(F32)).astype(BF16)

    load_o.wait()
    n_chunks = wo_v.shape[1] // N_CHUNK
    block = chips * toks
    pair_copies, red_copies = [], []

    def reduce_chunk(i):
        pair_copies[i].wait_recv()
        z[i] = y_mine[i] + y_rx[i]
        for j in range(1, chips):
            rows_j = pl.ds(pl.multiple_of(peer(j) * toks, toks), toks)
            red_copies.append(send(
                z.at[i, rows_j], z_rx.at[j - 1, i], red_send.at[j - 1, i], red_recv.at[j - 1, i], peer(j) * CORES + core
            ))

    for i in range(n_chunks):
        y = dot(split[...], wo_v[:, i * N_CHUNK:(i + 1) * N_CHUNK])
        y = (y[:all_toks] + y[all_toks:]).reshape(chips, CORES, toks, N_CHUNK)
        first, second = y[:, 0].reshape(block, N_CHUNK), y[:, 1].reshape(block, N_CHUNK)
        y_mine[i] = jnp.where(core == 0, first, second)
        y_out[i] = jnp.where(core == 0, second, first)
        pair_copies.append(send(y_out.at[i], y_rx.at[i], pair_send.at[i], pair_recv.at[i], mate))
        if i:
            reduce_chunk(i - 1)
    reduce_chunk(n_chunks - 1)
    own = pl.ds(pl.multiple_of(chip * toks, toks), toks)
    for i in range(n_chunks):
        y = z[i, own, :]
        for j in range(1, chips):
            red_copies[i * (chips - 1) + j - 1].wait_recv()
            y = y + z_rx[j - 1, i]
        out_ref[:, i * N_CHUNK:(i + 1) * N_CHUNK] = y.astype(BF16)

    for copy in [send_pre, send_pseg, send_new] + gathers + send_stats + pair_copies + red_copies:
        copy.wait_send()


def solution(mesh):
    n = mesh.shape["sp"]
    chips = n // CORES
    tok_spec = P(("dp", "sp"), None)
    vec_spec = P(("dp", "sp"))
    mat_spec = P(None, None)
    gain_spec = P(None)

    def device_step(hidden, seg_ids, positions, prefix_lat, prefix_seg, w_dq, gain_q, w_uq, w_dkv, gain_kv, w_ukv, w_o):
        toks, width = hidden.shape
        pre, lat_dim = prefix_lat.shape
        q_lat = w_dq.shape[1]
        kv_lat = w_ukv.shape[0]
        heads = w_o.shape[0] // V_DIM // CORES
        rows = CORES * (pre + toks)
        all_toks = n * toks
        n_chunks = width // N_CHUNK
        inv_freq = (ROPE_BASE ** (-np.arange(HALF, dtype=np.float64) / HALF)).astype(np.float32)
        freq = jnp.asarray(np.concatenate([inv_freq] * (LANES // HALF)).reshape(1, LANES))
        vmem = pl.BlockSpec(memory_space=pltpu.VMEM)
        hbm = pl.BlockSpec(memory_space=pl.ANY)
        dma = pltpu.SemaphoreType.DMA
        return pl.pallas_call(
            functools.partial(kernel, n),
            out_shape=jax.ShapeDtypeStruct((toks, width), BF16),
            in_specs=[vmem] * 6 + [hbm] * 7,
            out_specs=vmem,
            scratch_shapes=[
                pltpu.VMEM((toks, width), BF16),
                pltpu.VMEM((width, q_lat), BF16),
                pltpu.VMEM((width, lat_dim), BF16),
                pltpu.VMEM((q_lat, heads * QK_DIM), BF16),
                pltpu.VMEM((kv_lat, heads * KV_HEAD), BF16),
                pltpu.VMEM((heads * V_DIM, width), BF16),
                pltpu.VMEM((rows, lat_dim), BF16),
                pltpu.VMEM((1, pre), jnp.int32),
                pltpu.VMEM((all_toks, q_lat), BF16),
                pltpu.VMEM((all_toks, LANES), F32),
                pltpu.VMEM((rows, LANES), BF16),
                pltpu.VMEM((heads, rows, NOPE_DIM), BF16),
                pltpu.VMEM((heads, all_toks, 2 * LANES), BF16),
                pltpu.VMEM((heads, rows, all_toks), BF16),
                pltpu.VMEM((2 * heads, all_toks), F32),
                pltpu.VMEM((chips - 1, 2 * heads, all_toks), F32),
                pltpu.VMEM((all_toks, heads * V_DIM), F32),
                pltpu.VMEM((2 * all_toks, heads * V_DIM), BF16),
                pltpu.VMEM((CORES * toks, all_toks), F32),
                pltpu.VMEM((n_chunks, chips * toks, N_CHUNK), F32),
                pltpu.VMEM((n_chunks, chips * toks, N_CHUNK), F32),
                pltpu.VMEM((n_chunks, chips * toks, N_CHUNK), F32),
                pltpu.VMEM((n_chunks, chips * toks, N_CHUNK), F32),
                pltpu.VMEM((chips - 1, n_chunks, toks, N_CHUNK), F32),
                dma((6,)),
                dma((KV_LOADS,)),
                dma((3,)), dma((3,)),
                dma((n - 1,)), dma((n - 1,)),
                dma((n - 1,)), dma((n - 1,)),
                dma((chips - 1,)), dma((chips - 1,)),
                dma((n_chunks,)), dma((n_chunks,)),
                dma((chips - 1, n_chunks)), dma((chips - 1, n_chunks)),
            ],
            compiler_params=pltpu.CompilerParams(
                collective_id=0, has_side_effects=True, vmem_limit_bytes=60 * 1024 * 1024
            ),
        )(
            freq, seg_ids.reshape(1, toks), positions.reshape(1, toks), prefix_seg.reshape(1, pre),
            gain_q.reshape(1, q_lat), gain_kv.reshape(1, kv_lat),
            hidden, prefix_lat, w_dq, w_uq, w_dkv, w_ukv, w_o,
        )

    return jax.shard_map(
        device_step,
        mesh=mesh,
        in_specs=(tok_spec, vec_spec, vec_spec, tok_spec, vec_spec, mat_spec, gain_spec, mat_spec, mat_spec, gain_spec, mat_spec, mat_spec),
        out_specs=tok_spec,
        check_vma=False,
    )
```

time: 127 us -> 50.3 us (0.40)
  blocking collectives: 63.9 us -> 0 us
  Pallas kernels: 0 us -> 41.4 us
  matrix products: 33 us -> 0 us
  between operations: 14.2 us -> 0.01 us
  other arithmetic: 8 us -> 0 us
  local copies, waits for them, and re-layouts: 7.28 us -> 8.67 us
    all_gather x2 -> x0, blocking collectives: 44.8 us -> none  [the longest x1 23.2 us: device_step(): prefix_seg_all = lax.all_gather(prefix_seg, 'sp', axis=0, tiled=True)]
    pallas_call x0 -> x1, Pallas kernels: none -> 41.4 us  [device_step(): pl.pallas_call(functools.partial(kernel, n), out_shape=jax.ShapeDtypeStru...]
    dot_general x7 -> x0, matrix products: 31.6 us -> none  [the longest x1 10.3 us: head_attention(): jnp.einsum('kc,chd->khd', key_lat[:, :KV_LAT], w_ukv_part.reshape(KV_LAT,...]
    unnamed x1 -> x0, blocking collectives: 10.5 us -> none
    all_to_all x1 -> x0, blocking collectives: 8.65 us -> none  [device_step(): tok_out = lax.all_to_all(heads_out, 'sp', 0, 1, tiled=True)]
    sub x1 -> x0, other arithmetic: 4.81 us -> none  [attend(): probs = jax.nn.softmax(scores, axis=-1).astype(jnp.bfloat16)]
    reshape x0 -> x2, local copies, waits for them, and re-layouts: none -> 2.48 us  [the longest x1 1.26 us: device_step(): gain_kv.reshape(1, kv_lat)]
    convert_element_type x6 -> x0, other arithmetic: 2.18 us -> none  [the longest x2 1.36 us: rms_norm(): return values * inv_rms * gain.astype(jnp.float32)]
  transfers between devices with their start and end apart: 1 -> 0, of which waited for: 0 -> 0; matrix products, arithmetic and copies ran while one was open for 10% -> 0% of each run, Pallas kernels for 0% -> 0%
where the time goes in v1:
time: 50.3 us; the launch traced here: 50.1 us
  Pallas kernels  41.4 us (82%)
  local copies, waits for them, and re-layouts  8.67 us (17%)
    pallas_call x1, Pallas kernels, device_step(): pl.pallas_call(functools.partial(kernel, n), out_shape=jax.ShapeDtypeStru...  41.4 us
    unnamed x3, local copies, waits for them, and re-layouts  6.19 us
    reshape x1, local copies, waits for them, and re-layouts, device_step(): gain_kv.reshape(1, kv_lat)  1.26 us
    reshape x1, local copies, waits for them, and re-layouts, device_step(): gain_q.reshape(1, q_lat)  1.22 us

profile of v1, /device:TPU:112, one launch (start us, length us, event | category | flops | bytes accessed | tf_op | source)
XLA Modules:
  0.0 50.1 jit_solution(16323377563014642003)
XLA Ops:
  0.0 1.2 %reshape.18.gain_q_ref = bf16[1,384]{1,0:T(2,128)(2,1)} reshape(bf16[384]{0:T(512)(128)(2,1)} %param.19) | data formatting | bytes 1536 | tf_op jit(solution)/shard_map/reshape | solution.py:364
  1.2 1.3 %reshape.19.gain_kv_ref = bf16[1,512]{1,0:T(2,128)(2,1)} reshape(bf16[512]{0:T(512)(128)(2,1)} %param.22) | data formatting | bytes 2048 | tf_op jit(solution)/shard_map/reshape | solution.py:364
  2.5 2.1 %copy.14.pre_hbm = bf16[512,576]{1,0:T(8,128)(2,1)} copy(bf16[512,576]{0,1:T(8,128)(2,1)} %param.16) | data formatting | bytes 1179648 | tf_op args[3]
  4.6 2.6 %copy.15.wdkv_hbm = bf16[1280,576]{1,0:T(8,128)(2,1)} copy(bf16[1280,576]{0,1:T(8,128)(2,1)} %param.21) | data formatting | bytes 2949120 | tf_op args[8]
  7.3 41.4 %shard_map.127 = bf16[16,1280]{1,0:T(8,128)(2,1)} custom-call(f32[1,128]{1,0:T(1,128)} %constant.2.clone.freq_ref, s32[1,16]{1,0:T(1,128)} %bitcast.4, s32[1,16]{1,0:T(1,128)} %bitcast.5, s32[1,512]{1,0:T(1,128)} %bitcast.3, bf16[1,384]{1,0:T(2,128)(2,1)} %reshape.18.gain_q_ref, bf16[1,512]{1,0:T(2,128)(2,1)} %reshape.19.gain_kv_ref, ...), custom_call_target="tpu_custom_call" | custom-call | tf_op jit(solution)/shard_map/pallas_call | solution.py:320
  48.7 1.4 %copy.17 = bf16[16,1280]{1,0:T(8,128)(2,1)} copy(bf16[16,1280]{1,0:T(8,128)(2,1)} %shard_map.127) | data formatting | bytes 81920
